TPU v7x, 256 devices: a whole 4x4x8 slice. The times are simulated.
256 devices in a mesh: data: 256 (over z, y, x, core).
Axes of the slice: x: 4, y: 4, z: 8, core: 2. Of those that a mesh axis runs over, the one named last changes fastest.
Arguments:
- tokens: bfloat16 [131072, 768], P('data')
- labels: int32 [4, 131072], P(None, 'data')
- w_one: bfloat16 [768, 3072], replicated
- w_two: bfloat16 [3072, 768], replicated
- adapter_a: bfloat16 [768, 8], replicated
- adapter_b: bfloat16 [8, 3072], replicated
- task_heads: bfloat16 [4, 768, 3], replicated
Outputs:
- output 1: float32 [4], replicated
- output 2: float32 [768, 8], P('data')
- output 3: float32 [8, 3072], P(None, 'data')
All inputs are finite; a program needn't handle non-finite values.
Results may differ from a plain program's by a relative error of at most 0.001.
Values are sent between devices in bfloat16 or wider.
A program may use at most 768 MiB of HBM per device.

v0:
```python
import jax
import jax.numpy as jnp
from jax import lax
from jax.sharding import PartitionSpec as P

EG_STEPS = 20


def weight_solver(gram_mat):
    num_tasks = gram_mat.shape[0]
    eg_scale = jnp.trace(gram_mat) / num_tasks

    def eg_step(step_idx, weights):
        weights = weights * jnp.exp(-jnp.sum(gram_mat * weights[None, :], axis=1) / eg_scale)
        return weights / jnp.sum(weights)

    return lax.fori_loop(0, EG_STEPS, eg_step, jnp.full((num_tasks,), 1.0 / num_tasks, jnp.float32))


def task_grads(tokens, labels, w_one, w_two, adapter_a, adapter_b, task_heads):
    num_classes = task_heads.shape[2]
    low_rank = jnp.dot(tokens, adapter_a, preferred_element_type=jnp.float32).astype(jnp.bfloat16)
    pre_act = jnp.dot(tokens, w_one, preferred_element_type=jnp.float32) + jnp.dot(low_rank, adapter_b, preferred_element_type=jnp.float32)
    gelu_out, gelu_slope = jax.jvp(jax.nn.gelu, (pre_act,), (jnp.ones_like(pre_act),))
    hidden = gelu_out.astype(jnp.bfloat16)
    trunk_out = (tokens.astype(jnp.float32) + jnp.dot(hidden, w_two, preferred_element_type=jnp.float32)).astype(jnp.bfloat16)
    logits = jnp.einsum("bd,tdc->tbc", trunk_out, task_heads, preferred_element_type=jnp.float32)
    task_probs = jax.nn.softmax(logits, axis=-1)
    onehot = (labels[:, :, None] == jnp.arange(num_classes)[None, None, :]).astype(jnp.float32)
    logit_err = (task_probs - onehot).astype(jnp.bfloat16)
    d_trunk = jnp.einsum("tbc,tdc->tbd", logit_err, task_heads, preferred_element_type=jnp.float32).astype(jnp.bfloat16)
    d_hidden = jnp.einsum("tbd,fd->tbf", d_trunk, w_two, preferred_element_type=jnp.float32)
    d_pre = (d_hidden * gelu_slope[None]).astype(jnp.bfloat16)
    part_b = jnp.einsum("cs,ucg->usg", low_rank, d_pre, preferred_element_type=jnp.float32)
    d_low = jnp.einsum("tbf,rf->tbr", d_pre, adapter_b, preferred_element_type=jnp.float32).astype(jnp.bfloat16)
    part_a = jnp.einsum("bd,tbr->tdr", tokens, d_low, preferred_element_type=jnp.float32)
    return part_a, part_b


def solution(mesh):
    num_dev = mesh.shape["data"]

    def device_step(tokens, labels, w_one, w_two, adapter_a, adapter_b, task_heads):
        batch_total = tokens.shape[0] * num_dev
        part_a, part_b = task_grads(tokens, labels, w_one, w_two, adapter_a, adapter_b, task_heads)
        shard_a = lax.psum_scatter(part_a, "data", scatter_dimension=1, tiled=True) / batch_total
        shard_b = lax.psum_scatter(part_b, "data", scatter_dimension=2, tiled=True) / batch_total
        gram_part = jnp.einsum("tdr,sdr->ts", shard_a, shard_a, precision=lax.Precision.HIGHEST) + jnp.einsum("usg,tsg->ut", shard_b, shard_b, precision=lax.Precision.HIGHEST)
        gram_mat = lax.psum(gram_part, "data")
        task_weights = weight_solver(gram_mat)
        comb_a = jnp.sum(task_weights[:, None, None] * shard_a, axis=0)
        comb_b = jnp.sum(task_weights[:, None, None] * shard_b, axis=0)
        return task_weights, comb_a, comb_b

    return jax.shard_map(device_step, mesh=mesh, in_specs=(P("data", None), P(None, "data"), P(), P(), P(), P(), P()), out_specs=(P(), P("data", None), P(None, "data")), check_vma=False)
```

profile of v0, /device:TPU:1, one launch (start us, length us, event | category | flops | bytes accessed | tf_op | source)
XLA Modules:
  0.0 451.1 jit_solution(13085647389173569005)
XLA Ops:
  7.2 1.4 convolution_convert_fusion.1
  8.7 4.7 %fusion.45 = f32[512,3072]{1,0:T(8,128)S(1)} fusion(bf16[512,768]{1,0:T(8,128)(2,1)} %param.9, bf16[768,3072]{1,0:T(8,128)(2,1)} %param.11), kind=kOutput, calls=%fused_computation.62 | convolution fusion | flops 2415919104 | bytes 11796480 | tf_op jit(solution)/shard_map/dot_general | solution.py:23
  13.4 6.9 %fusion.9 = (f32[512,3072]{1,0:T(8,128)}, f32[512,3072]{1,0:T(8,128)}) fusion(f32[512,3072]{1,0:T(8,128)S(1)} %fusion.45, bf16[512,8]{0,1:T(8,128)(2,1)S(1)} %convolution_convert_fusion.1, bf16[8,3072]{1,0:T(8,128)(2,1)S(1)} %copy-done), kind=kOutput, calls=%fused_computation.16 | convolution fusion | flops 51904512 | bytes 18931712 | tf_op jit(solution)/shard_map/dot_general | solution.py:23
  20.3 8.2 %fusion.44 = (f32[4,512]{1,0:T(4,128)S(1)}, f32[4,512,3]{1,0,2:T(4,128)S(1)}) fusion(bf16[4,768,3]{1,0,2:T(4,128)(2,1)S(1)} %copy-done.4, bf16[3072,768]{1,0:T(8,128)(2,1)} %param.12, f32[512,3072]{1,0:T(8,128)} %get-tuple-element.57, bf16[512,768]{1,0:T(8,128)(2,1)S(1)} %copy-done.1), kind=kOutput, calls=%fused_computation.61 | convolution fusion | flops 2440695808 | bytes 11847680 | tf_op jit(solution)/shard_map/bd,tdc->tbc/dot_general | solution.py:27
  28.5 17.2 %multiply_convert_fusion = bf16[4,512,3072]{2,1,0:T(8,128)(2,1)} fusion(f32[512,3072]{1,0:T(8,128)} %get-tuple-element.56, bf16[3072,768]{1,0:T(8,128)(2,1)} %param.12, bf16[4,768,3]{1,0,2:T(4,128)(2,1)S(1)} %copy-done.4, bf16[4,512,3]{1,0,2:T(4,128)(2,1)S(1)} %fusion.24), kind=kOutput, calls=%fused_computation.4 | convolution fusion | flops 9687269376 | bytes 23623680 | tf_op jit(solution)/shard_map/tbd,fd->tbf/dot_general | solution.py:32
  45.7 7.7 %convolution_bitcast_fusion = f32[4,8,3072]{2,1,0:T(8,128)} fusion(bf16[4,512,3072]{2,1,0:T(8,128)(2,1)} %multiply_convert_fusion, bf16[512,8]{0,1:T(8,128)(2,1)S(1)} %convolution_convert_fusion.1), kind=kOutput, calls=%fused_computation.20 | convolution fusion | flops 100663296 | bytes 12984320 | tf_op jit(solution)/shard_map/cs,ucg->usg/dot_general | solution.py:34
  53.4 8.1 %convolution_bitcast_fusion.1 = f32[4,768,8]{1,2,0:T(8,128)S(1)} fusion(bf16[4,512,3072]{2,1,0:T(8,128)(2,1)} %multiply_convert_fusion, bf16[512,768]{1,0:T(8,128)(2,1)S(1)} %copy-done.1, bf16[8,3072]{1,0:T(8,128)(2,1)S(1)} %copy-done), kind=kOutput, calls=%fused_computation.27 | convolution fusion | flops 125845504 | bytes 13516800 | tf_op jit(solution)/shard_map/bd,tbr->tdr/dot_general | solution.py:36
  61.5 1.5 copy.14
  63.0 269.2 %all-reduce.5.cloned.1.call-done = (f32[4,8,3072]{2,1,0:T(8,128)}, f32[4,768,8]{2,0,1:T(4,128)}) async-done(((f32[4,8,3072]{2,1,0:T(8,128)}, f32[4,768,8]{2,0,1:T(4,128)}), (f32[4,8,3072]{2,1,0:T(8,128)}, f32[4,768,8]{2,0,1:T(4,128)})) %all-reduce.5.cloned.1.call-update) | async-done | bytes 491536
  332.2 0.8 dynamic-slice_multiply_fusion
  333.2 0.9 fusion.18
  334.1 77.6 %psum.7 = f32[4,4]{1,0:T(4,128)S(1)} all-reduce(f32[4,4]{1,0:T(4,128)S(1)} %fusion.18), channel_id=1, replica_groups=mesh['data'=256] {'data'}, use_global_device_ids=true, to_apply=%region_4.0 | all-reduce | flops 16 | bytes 128 | tf_op jit(solution)/shard_map/psum | solution.py:49
  413.0 28.4 %while.11 = (s32[]{:T(128)}, f32[4]{0:T(128)S(1)}, f32[4,4]{1,0:T(4,128)S(1)}, f32[]{:T(128)}, s32[]{:T(128)}, /*index=5*/s32[]{:T(128)}) while((s32[]{:T(128)}, f32[4]{0:T(128)S(1)}, f32[4,4]{1,0:T(4,128)S(1)}, f32[]{:T(128)}, s32[]{:T(128)}, /*index=5*/s32[]{:T(128)}) %tuple.32), condition=%wide.region_9.10_spmd.clone, body=%wide.region_6.9_spmd.clone.sunk | while | flops 58 | bytes 300 | solution.py:17
  413.2 0.6 fusion.57
  413.8 0.6 broadcast_divide_fusion.2
  414.6 0.6 fusion.57
  415.2 0.6 broadcast_divide_fusion.2
  416.6 0.6 broadcast_divide_fusion.2
  417.4 0.6 fusion.57
  418.0 0.6 broadcast_divide_fusion.2
  418.8 0.6 fusion.57
  419.4 0.6 broadcast_divide_fusion.2
  420.9 0.6 broadcast_divide_fusion.2
  421.7 0.6 fusion.57
  422.3 0.6 broadcast_divide_fusion.2
  423.1 0.6 fusion.57
  423.7 0.6 broadcast_divide_fusion.2
  424.5 0.6 fusion.57
  425.1 0.6 broadcast_divide_fusion.2
  425.9 0.6 fusion.57
  426.5 0.6 broadcast_divide_fusion.2
  427.3 0.6 fusion.57
  428.0 0.6 broadcast_divide_fusion.2
  428.8 0.6 fusion.57
  429.4 0.6 broadcast_divide_fusion.2
  430.8 0.6 broadcast_divide_fusion.2
  431.6 0.6 fusion.57
  432.2 0.6 broadcast_divide_fusion.2
  433.0 0.6 fusion.57
  433.6 0.6 broadcast_divide_fusion.2
  435.1 0.6 broadcast_divide_fusion.2
  435.9 0.6 fusion.57
  436.5 0.6 broadcast_divide_fusion.2
  437.9 0.6 broadcast_divide_fusion.2
  439.3 0.6 broadcast_divide_fusion.2
  440.7 0.6 broadcast_divide_fusion.2
  441.4 1.4 multiply_reduce_fusion.1
  442.9 1.4 multiply_reduce_fusion.2
  (65 shorter events, 7.6 us)
Async XLA Ops:
  7.2 6.2 %copy-start = (bf16[8,3072]{1,0:T(8,128)(2,1)S(1)}, bf16[8,3072]{1,0:T(8,128)(2,1)}, u32[]{:S(2)}) copy-start(bf16[8,3072]{1,0:T(8,128)(2,1)} %param.14) | copy-start | bytes 147460
  7.2 325.1 %all-reduce.5.cloned.1.call-start = ((), (), s32[]{:S(2)}) async-start(), calls=%async_computation | async-start | bytes 3932160
  13.3 6.9 %copy-start.1 = (bf16[512,768]{1,0:T(8,128)(2,1)S(1)}, bf16[512,768]{1,0:T(8,128)(2,1)}, u32[]{:S(2)}) copy-start(bf16[512,768]{1,0:T(8,128)(2,1)} %param.9) | copy-start | bytes 2359300
  13.4 6.9 %copy-start.4 = (bf16[4,768,3]{1,0,2:T(4,128)(2,1)S(1)}, bf16[4,768,3]{1,0,2:T(4,128)(2,1)}, u32[]{:S(2)}) copy-start(bf16[4,768,3]{1,0,2:T(4,128)(2,1)} %param.15) | copy-start | bytes 55300
  20.3 8.2 %copy-start.3 = (s32[4,512]{1,0:T(4,128)S(1)}, s32[4,512]{1,0:T(4,128)}, u32[]{:S(2)}) copy-start(s32[4,512]{1,0:T(4,128)} %param.10) | copy-start | bytes 24580
  441.4 2.8 copy-start.2
Sparse Core Ops, SparseCore 0:
  63.1 269.1 all-reduce.4
where the time goes:
time: 452 us; the launch traced here: 451 us
  waiting for transfers between devices  269 us (60%)
  blocking collectives  77.6 us (17%)
  matrix products  55.2 us (12%)
  other arithmetic  32 us (7%)
  between operations  14.8 us (3%)
    unnamed x2, waiting for transfers between devices  269 us
    psum x1, blocking collectives, device_step(): gram_mat = lax.psum(gram_part, 'data')  77.6 us
    dot_general x1, matrix products, task_grads(): jnp.einsum('tbd,fd->tbf', d_trunk, w_two, preferred_element_type=jnp.floa...  17.2 us
    div x20, other arithmetic, eg_step(): return weights / jnp.sum(weights)  13 us
    reduce_sum x20, other arithmetic, eg_step(): return weights / jnp.sum(weights)  12.4 us
  transfers between devices with their start and end apart: 1, of which 1 were waited for; matrix products, arithmetic and copies ran while one was open for 0% of the time, Pallas kernels for 0%

commit v1 on v0

v1 whole, which is shorter than its diff:
```python
import functools

import jax
import jax.numpy as jnp
from jax import lax
from jax.experimental import pallas as pl
from jax.experimental.pallas import tpu as pltpu
from jax.sharding import PartitionSpec as P

EG_STEPS = 20
AXIS = "data"
DIMS = (8, 4, 4, 2)
LANES = 128
MESH_ID = pl.DeviceIdType.MESH


def task_grads(tokens, labels, w_one, w_two, adapter_a, adapter_b, task_heads):
    num_classes = task_heads.shape[2]
    low_rank = jnp.dot(tokens, adapter_a, preferred_element_type=jnp.float32).astype(jnp.bfloat16)
    pre_act = jnp.dot(tokens, w_one, preferred_element_type=jnp.float32) + jnp.dot(low_rank, adapter_b, preferred_element_type=jnp.float32)
    gelu_out, gelu_slope = jax.jvp(jax.nn.gelu, (pre_act,), (jnp.ones_like(pre_act),))
    hidden = gelu_out.astype(jnp.bfloat16)
    trunk_out = (tokens.astype(jnp.float32) + jnp.dot(hidden, w_two, preferred_element_type=jnp.float32)).astype(jnp.bfloat16)
    logits = jnp.einsum("bd,tdc->tbc", trunk_out, task_heads, preferred_element_type=jnp.float32)
    task_probs = jax.nn.softmax(logits, axis=-1)
    onehot = (labels[:, :, None] == jnp.arange(num_classes)[None, None, :]).astype(jnp.float32)
    logit_err = (task_probs - onehot).astype(jnp.bfloat16)
    d_trunk = jnp.einsum("tbc,tdc->tbd", logit_err, task_heads, preferred_element_type=jnp.float32).astype(jnp.bfloat16)
    d_hidden = jnp.einsum("tbd,fd->tbf", d_trunk, w_two, preferred_element_type=jnp.float32)
    d_pre = (d_hidden * gelu_slope[None]).astype(jnp.bfloat16)
    part_b = jnp.einsum("cs,ucg->usg", low_rank, d_pre, preferred_element_type=jnp.float32)
    d_low = jnp.einsum("tbf,rf->tbr", d_pre, adapter_b, preferred_element_type=jnp.float32).astype(jnp.bfloat16)
    part_a = jnp.einsum("bd,tbr->trd", tokens, d_low, preferred_element_type=jnp.float32)
    return part_a, part_b


def remote(src, dst, send_sem, recv_sem, dev):
    return pltpu.make_async_remote_copy(src_ref=src, dst_ref=dst, send_sem=send_sem, recv_sem=recv_sem, device_id=(dev,), device_id_type=MESH_ID)


def exchange_kernel(dims, tasks, batch_total, pb_ref, pa_ref, alpha_ref, ga_ref, gb_ref, pk, swap, mine, rs, xs, gram, swap_s, swap_r, rs_s, rs_r, x_s, x_r, g_s, g_r):
    dim_z, dim_y, dim_x, _ = dims
    num_q = dim_z * dim_y
    rank = pb_ref.shape[0] // tasks
    half = pb_ref.shape[0] // 2
    wide_b = pb_ref.shape[1] // num_q
    wide_a = pa_ref.shape[1] // num_q
    own_b = wide_b // (dim_x * 2)
    own_a = wide_a // (dim_x * 2)

    me = lax.axis_index(AXIS)
    core = lax.rem(me, 2)
    x_pos = lax.rem(me // 2, dim_x)
    q_pos = me // (2 * dim_x)
    y_pos = lax.rem(q_pos, dim_y)
    z_pos = q_pos // dim_y

    def dev(q, x, c):
        return (q * dim_x + x) * 2 + c

    offsets = [(dz, dy) for dz in range(dim_z) for dy in range(dim_y)]
    offsets.sort(key=lambda o: -(min(o[0], dim_z - o[0]) + min(o[1], dim_y - o[1])))
    ahead = [lax.rem(z_pos + dz, dim_z) * dim_y + lax.rem(y_pos + dy, dim_y) for dz, dy in offsets]
    partner = dev(q_pos, x_pos, 1 - core)
    row_peers = [(kx, kc) for kx in range(dim_x) for kc in range(2) if (kx, kc) != (0, 0)]

    def row_dev(kx, kc):
        return dev(q_pos, lax.rem(x_pos + kx, dim_x), lax.rem(core + kc, 2))

    barrier = pltpu.get_barrier_semaphore()
    for s in range(num_q - 1):
        pl.semaphore_signal(barrier, inc=1, device_id=(dev(ahead[s], x_pos, core),), device_id_type=MESH_ID)
    for kx, kc in row_peers:
        pl.semaphore_signal(barrier, inc=1, device_id=(row_dev(kx, kc),), device_id_type=MESH_ID)

    for q in range(num_q):
        chunk = jnp.concatenate(
            [
                pb_ref[:, q * wide_b : (q + 1) * wide_b],
                pa_ref[:, q * wide_a : (q + 1) * wide_a],
                jnp.zeros((2 * half, LANES - wide_a - wide_b), jnp.float32),
            ],
            axis=1,
        )
        pk[0, q] = chunk[:half]
        pk[1, q] = chunk[half:]

    pl.semaphore_wait(barrier, num_q - 1 + len(row_peers))

    swaps = [remote(pk.at[1 - core, ahead[s]], swap.at[s], swap_s.at[s], swap_r.at[s], partner) for s in range(num_q)]
    for copy in swaps:
        copy.start()
    sends = []
    for s in range(num_q):
        swaps[s].wait_recv()
        mine[s] = pk[core, ahead[s]] + swap[s]
        if s < num_q - 1:
            copy = remote(mine.at[s], rs.at[s], rs_s.at[s], rs_r.at[s], dev(ahead[s], x_pos, core))
            copy.start()
            sends.append(copy)
    acc = mine[num_q - 1]
    for s in reversed(range(num_q - 1)):
        sends[s].wait_recv()
        acc = acc + rs[s]

    xs[core, x_pos] = acc
    for i, (kx, kc) in enumerate(row_peers):
        copy = remote(xs.at[core, x_pos], xs.at[core, x_pos], x_s.at[i], x_r.at[core, x_pos], row_dev(kx, kc))
        copy.start()
        sends.append(copy)
    for i, (kx, kc) in enumerate(row_peers):
        cc, xx = lax.rem(core + kc, 2), lax.rem(x_pos + kx, dim_x)
        remote(xs.at[cc, xx], xs.at[cc, xx], x_s.at[i], x_r.at[cc, xx], row_dev(kx, kc)).wait_recv()
    grads = []
    for c in range(2):
        both = xs[c, 0]
        for i in range(1, dim_x):
            both = both + xs[c, i]
        both = both * (1.0 / batch_total)
        for t in range(tasks // 2):
            grads.append(both[t * rank : (t + 1) * rank])

    lane = lax.broadcasted_iota(jnp.int32, (1, LANES), 1)
    pairs = [(t, s) for t in range(tasks) for s in range(t, tasks)]
    row = jnp.zeros((1, LANES), jnp.float32)
    for i, (t, s) in enumerate(pairs):
        dot = jnp.sum(jnp.sum(grads[t] * grads[s], axis=0, keepdims=True), axis=1, keepdims=True)
        row = jnp.where(lane == i, dot, row)
    gram[q_pos] = row
    for s in range(num_q - 1):
        copy = remote(gram.at[q_pos], gram.at[q_pos], g_s.at[s], g_r.at[q_pos], dev(ahead[s], x_pos, core))
        copy.start()
        sends.append(copy)
    for s in range(num_q - 1):
        remote(gram.at[ahead[s]], gram.at[ahead[s]], g_s.at[s], g_r.at[ahead[s]], dev(ahead[s], x_pos, core)).wait_recv()
    row = gram[0]
    for q in range(1, num_q):
        row = row + gram[q]
    mat = {}
    for i, (t, s) in enumerate(pairs):
        val = jnp.sum(jnp.where(lane == i, row, 0.0), axis=1, keepdims=True)
        mat[t, s] = mat[s, t] = jnp.broadcast_to(val, (1, LANES))
    scale = mat[0, 0]
    for t in range(1, tasks):
        scale = scale + mat[t, t]
    scale = scale / tasks
    weights = tuple(jnp.full((1, LANES), 1.0 / tasks, jnp.float32) for _ in range(tasks))

    def eg_step(_, weights):
        new = []
        for t in range(tasks):
            dot = mat[t, 0] * weights[0]
            for s in range(1, tasks):
                dot = dot + mat[t, s] * weights[s]
            new.append(weights[t] * jnp.exp(-dot / scale))
        total = new[0]
        for t in range(1, tasks):
            total = total + new[t]
        return tuple(w / total for w in new)

    weights = lax.fori_loop(0, EG_STEPS, eg_step, weights)
    row = jnp.zeros((1, LANES), jnp.float32)
    comb = jnp.zeros((rank, LANES), jnp.float32)
    for t in range(tasks):
        row = jnp.where(lane == t, weights[t], row)
        comb = comb + weights[t] * grads[t]
    alpha_ref[...] = row[:, :tasks]
    place = x_pos * 2 + core
    gb_ref[...] = pltpu.roll(comb, lax.rem(LANES - place * own_b, LANES), 1)[:, :own_b]
    ga_ref[...] = jnp.transpose(pltpu.roll(comb, LANES - wide_b - place * own_a, 1))[:own_a]
    for copy in swaps + sends:
        copy.wait_send()


def exchange(part_b, part_a, dims, tasks, batch_total):
    num_dev = 2 * dims[0] * dims[1] * dims[2]
    num_q = dims[0] * dims[1]
    rank = part_b.shape[0] // tasks
    half = part_b.shape[0] // 2
    slab = (half, LANES)
    dma = pltpu.SemaphoreType.DMA
    return pl.pallas_call(
        functools.partial(exchange_kernel, dims, tasks, batch_total),
        out_shape=(
            jax.ShapeDtypeStruct((1, tasks), jnp.float32),
            jax.ShapeDtypeStruct((part_a.shape[1] // num_dev, rank), jnp.float32),
            jax.ShapeDtypeStruct((rank, part_b.shape[1] // num_dev), jnp.float32),
        ),
        in_specs=[pl.BlockSpec(memory_space=pltpu.VMEM)] * 2,
        out_specs=[pl.BlockSpec(memory_space=pltpu.VMEM)] * 3,
        scratch_shapes=[
            pltpu.VMEM((2, num_q) + slab, jnp.float32),
            pltpu.VMEM((num_q,) + slab, jnp.float32),
            pltpu.VMEM((num_q,) + slab, jnp.float32),
            pltpu.VMEM((num_q,) + slab, jnp.float32),
            pltpu.VMEM((2, dims[2]) + slab, jnp.float32),
            pltpu.VMEM((num_q, 1, LANES), jnp.float32),
            dma((num_q,)),
            dma((num_q,)),
            dma((num_q,)),
            dma((num_q,)),
            dma((2 * dims[2],)),
            dma((2, dims[2])),
            dma((num_q,)),
            dma((num_q,)),
        ],
        compiler_params=pltpu.CompilerParams(collective_id=0, has_side_effects=True),
        name="exchange",
    )(part_b, part_a)


def solution(mesh):
    num_dev = mesh.shape[AXIS]

    def device_step(tokens, labels, w_one, w_two, adapter_a, adapter_b, task_heads):
        batch_total = tokens.shape[0] * num_dev
        tasks = task_heads.shape[0]
        part_a, part_b = task_grads(tokens, labels, w_one, w_two, adapter_a, adapter_b, task_heads)
        part_a = part_a.reshape(-1, part_a.shape[2])
        part_b = part_b.reshape(-1, part_b.shape[2])
        alpha, grad_a, grad_b = exchange(part_b, part_a, DIMS, tasks, batch_total)
        return alpha.reshape(tasks), grad_a, grad_b

    return jax.shard_map(device_step, mesh=mesh, in_specs=(P(AXIS, None), P(None, AXIS), P(), P(), P(), P(), P()), out_specs=(P(), P(AXIS, None), P(None, AXIS)), check_vma=False)
```

time: 452 us -> 93.6 us (0.21)
  waiting for transfers between devices: 269 us -> 0 us
  blocking collectives: 77.6 us -> 0 us
  Pallas kernels: 0 us -> 34.1 us
  other arithmetic: 32 us -> 0.05 us
  between operations: 14.8 us -> 0.71 us
    unnamed x2 -> x0, waiting for transfers between devices: 269 us -> none
    psum x1 -> x0, blocking collectives: 77.6 us -> none  [device_step(): gram_mat = lax.psum(gram_part, 'data')]
    pallas_call x0 -> x1, Pallas kernels: none -> 34.1 us  [exchange(): pl.pallas_call(functools.partial(exchange_kernel, dims, tasks, batch_tota...]
    reduce_sum x43 -> x0, other arithmetic: 18.1 us -> none  [the longest x20 12.4 us: eg_step(): return weights / jnp.sum(weights)]
    div x21 -> x0, other arithmetic: 13.8 us -> none  [the longest x20 13 us: eg_step(): return weights / jnp.sum(weights)]
    dot_general x3 -> x1, matrix products: 9.17 us -> 8.73 us  [task_grads(): jnp.einsum('bd,tbr->trd', tokens, d_low, preferred_element_type=jnp.float32)]
  transfers between devices with their start and end apart: 1 -> 0, of which waited for: 1 -> 0; matrix products, arithmetic and copies ran while one was open for 0% -> 0% of each run, Pallas kernels for 0% -> 0%
where the time goes in v1:
time: 93.6 us; the launch traced here: 93.3 us
  matrix products  54.8 us (59%)
  Pallas kernels  34.1 us (36%)
  local copies, waits for them, and re-layouts  3.68 us (4%)
    pallas_call x1, Pallas kernels, exchange(): pl.pallas_call(functools.partial(exchange_kernel, dims, tasks, batch_tota...  34.1 us
    dot_general x1, matrix products, task_grads(): jnp.einsum('tbd,fd->tbf', d_trunk, w_two, preferred_element_type=jnp.floa...  17.3 us
    dot_general x1, matrix products, task_grads(): jnp.einsum('bd,tbr->trd', tokens, d_low, preferred_element_type=jnp.float32)  8.73 us
    dot_general x1, matrix products, task_grads(): jnp.einsum('bd,tdc->tbc', trunk_out, task_heads, preferred_element_type=j...  8.17 us
    dot_general x1, matrix products, task_grads(): jnp.einsum('cs,ucg->usg', low_rank, d_pre, preferred_element_type=jnp.flo...  7.67 us
    dot_general x1, matrix products, task_grads(): jnp.dot(low_rank, adapter_b, preferred_element_type=jnp.float32)  6.86 us
    dot_general x1, matrix products, task_grads(): jnp.dot(tokens, w_one, preferred_element_type=jnp.float32)  4.67 us
    unnamed x11, local copies, waits for them, and re-layouts  3.68 us

profile of v1, /device:TPU:1, one launch (start us, length us, event | category | flops | bytes accessed | tf_op | source)
XLA Modules:
  0.0 93.3 jit_solution(10191198065841461453)
XLA Ops:
  0.6 0.0 copy-start
  0.6 1.4 %convolution_convert_fusion.1 = bf16[512,8]{0,1:T(8,128)(2,1)S(1)} fusion(bf16[512,768]{1,0:T(8,128)(2,1)} %param.7, bf16[768,8]{0,1:T(8,128)(2,1)} %param.11), kind=kOutput, calls=%fused_computation.26 | convolution fusion | flops 6295552 | bytes 806912 | tf_op jit(solution)/shard_map/dot_general | solution.py:19
  2.1 4.7 %fusion.37 = f32[512,3072]{1,0:T(8,128)S(1)} fusion(bf16[512,768]{1,0:T(8,128)(2,1)} %param.7, bf16[768,3072]{1,0:T(8,128)(2,1)} %param.9), kind=kOutput, calls=%fused_computation.42 | convolution fusion | flops 2415919104 | bytes 11796480 | tf_op jit(solution)/shard_map/dot_general | solution.py:20
  6.8 0.0 copy-done
  6.8 0.0 copy-start.1
  6.8 0.0 copy-start.3
  6.8 6.9 %fusion.9 = (f32[512,3072]{1,0:T(8,128)}, f32[512,3072]{1,0:T(8,128)}) fusion(f32[512,3072]{1,0:T(8,128)S(1)} %fusion.37, bf16[512,8]{0,1:T(8,128)(2,1)S(1)} %convolution_convert_fusion.1, bf16[8,3072]{1,0:T(8,128)(2,1)S(1)} %copy-done), kind=kOutput, calls=%fused_computation.12 | convolution fusion | flops 51904512 | bytes 18931712 | tf_op jit(solution)/shard_map/dot_general | solution.py:20
  13.7 0.0 copy-done.1
  13.7 0.0 copy-done.3
  13.7 0.0 copy-start.2
  13.7 8.2 %fusion.36 = (f32[4,512]{1,0:T(4,128)S(1)}, f32[4,512,3]{1,0,2:T(4,128)S(1)}) fusion(bf16[4,768,3]{1,0,2:T(4,128)(2,1)S(1)} %copy-done.3, bf16[3072,768]{1,0:T(8,128)(2,1)} %param.10, f32[512,3072]{1,0:T(8,128)} %get-tuple-element.10, bf16[512,768]{1,0:T(8,128)(2,1)S(1)} %copy-done.1), kind=kOutput, calls=%fused_computation.41 | convolution fusion | flops 2440695808 | bytes 11847680 | tf_op jit(solution)/shard_map/bd,tdc->tbc/dot_general | solution.py:24
  21.9 0.0 copy-done.2
  21.9 17.3 %multiply_convert_fusion = bf16[4,512,3072]{2,1,0:T(8,128)(2,1)} fusion(f32[512,3072]{1,0:T(8,128)} %get-tuple-element.9, bf16[3072,768]{1,0:T(8,128)(2,1)} %param.10, bf16[4,768,3]{1,0,2:T(4,128)(2,1)S(1)} %copy-done.3, bf16[4,512,3]{1,0,2:T(4,128)(2,1)S(1)} %fusion.23), kind=kOutput, calls=%fused_computation | convolution fusion | flops 9687269376 | bytes 23623680 | tf_op jit(solution)/shard_map/tbd,fd->tbf/dot_general | solution.py:29
  39.2 8.7 %convolution_bitcast_fusion.1.pa_ref = f32[32,768]{1,0:T(8,128)} fusion(bf16[4,512,3072]{2,1,0:T(8,128)(2,1)} %multiply_convert_fusion, bf16[512,768]{1,0:T(8,128)(2,1)S(1)} %copy-done.1, bf16[8,3072]{1,0:T(8,128)(2,1)S(1)} %copy-done), kind=kOutput, calls=%fused_computation.23 | convolution fusion | flops 125845504 | bytes 13516800 | tf_op jit(solution)/shard_map/bd,tbr->trd/dot_general | solution.py:33
  47.9 7.7 %convolution_bitcast_fusion.pb_ref = f32[32,3072]{1,0:T(8,128)} fusion(bf16[4,512,3072]{2,1,0:T(8,128)(2,1)} %multiply_convert_fusion, bf16[512,8]{0,1:T(8,128)(2,1)S(1)} %convolution_convert_fusion.1), kind=kOutput, calls=%fused_computation.16 | convolution fusion | flops 100663296 | bytes 12984320 | tf_op jit(solution)/shard_map/cs,ucg->usg/dot_general | solution.py:31
  55.6 34.1 %exchange.1 = (f32[1,4]{1,0:T(1,128)}, f32[3,8]{1,0:T(4,128)}, f32[8,12]{1,0:T(8,128)}) custom-call(f32[32,3072]{1,0:T(8,128)} %convolution_bitcast_fusion.pb_ref, f32[32,768]{1,0:T(8,128)} %convolution_bitcast_fusion.1.pa_ref), custom_call_target="tpu_custom_call" | custom-call | tf_op jit(solution)/shard_map/exchange/pallas_call | solution.py:182
  89.7 1.1 %copy.21 = f32[4]{0:T(128)} copy(f32[4]{0:T(128)} %bitcast.40) | data formatting | bytes 32
  90.8 1.2 %copy.22 = f32[3,8]{1,0:T(4,128)} copy(f32[3,8]{1,0:T(4,128)} %get-tuple-element.17) | data formatting | bytes 192
  92.1 1.3 %copy.23 = f32[8,12]{1,0:T(8,128)} copy(f32[8,12]{1,0:T(8,128)} %get-tuple-element.18) | data formatting | bytes 768
  (2 shorter events, 0.1 us)
Async XLA Ops:
  0.6 6.1 %copy-start = (bf16[8,3072]{1,0:T(8,128)(2,1)S(1)}, bf16[8,3072]{1,0:T(8,128)(2,1)}, u32[]{:S(2)}) copy-start(bf16[8,3072]{1,0:T(8,128)(2,1)} %param.12) | copy-start | bytes 147460
  6.8 6.9 %copy-start.1 = (bf16[512,768]{1,0:T(8,128)(2,1)S(1)}, bf16[512,768]{1,0:T(8,128)(2,1)}, u32[]{:S(2)}) copy-start(bf16[512,768]{1,0:T(8,128)(2,1)} %param.7) | copy-start | bytes 2359300
  6.8 6.9 %copy-start.3 = (bf16[4,768,3]{1,0,2:T(4,128)(2,1)S(1)}, bf16[4,768,3]{1,0,2:T(4,128)(2,1)}, u32[]{:S(2)}) copy-start(bf16[4,768,3]{1,0,2:T(4,128)(2,1)} %param.13) | copy-start | bytes 55300
  13.7 8.2 %copy-start.2 = (s32[4,512]{1,0:T(4,128)S(1)}, s32[4,512]{1,0:T(4,128)}, u32[]{:S(2)}) copy-start(s32[4,512]{1,0:T(4,128)} %param.8) | copy-start | bytes 24580

commit v2 on v1

--- a/solution.py
+++ b/solution.py
@@ -14,24 +14,115 @@
 MESH_ID = pl.DeviceIdType.MESH
 
 
-def task_grads(tokens, labels, w_one, w_two, adapter_a, adapter_b, task_heads):
-    num_classes = task_heads.shape[2]
-    low_rank = jnp.dot(tokens, adapter_a, preferred_element_type=jnp.float32).astype(jnp.bfloat16)
-    pre_act = jnp.dot(tokens, w_one, preferred_element_type=jnp.float32) + jnp.dot(low_rank, adapter_b, preferred_element_type=jnp.float32)
-    gelu_out, gelu_slope = jax.jvp(jax.nn.gelu, (pre_act,), (jnp.ones_like(pre_act),))
-    hidden = gelu_out.astype(jnp.bfloat16)
-    trunk_out = (tokens.astype(jnp.float32) + jnp.dot(hidden, w_two, preferred_element_type=jnp.float32)).astype(jnp.bfloat16)
-    logits = jnp.einsum("bd,tdc->tbc", trunk_out, task_heads, preferred_element_type=jnp.float32)
-    task_probs = jax.nn.softmax(logits, axis=-1)
-    onehot = (labels[:, :, None] == jnp.arange(num_classes)[None, None, :]).astype(jnp.float32)
-    logit_err = (task_probs - onehot).astype(jnp.bfloat16)
-    d_trunk = jnp.einsum("tbc,tdc->tbd", logit_err, task_heads, preferred_element_type=jnp.float32).astype(jnp.bfloat16)
-    d_hidden = jnp.einsum("tbd,fd->tbf", d_trunk, w_two, preferred_element_type=jnp.float32)
-    d_pre = (d_hidden * gelu_slope[None]).astype(jnp.bfloat16)
-    part_b = jnp.einsum("cs,ucg->usg", low_rank, d_pre, preferred_element_type=jnp.float32)
-    d_low = jnp.einsum("tbf,rf->tbr", d_pre, adapter_b, preferred_element_type=jnp.float32).astype(jnp.bfloat16)
-    part_a = jnp.einsum("bd,tbr->trd", tokens, d_low, preferred_element_type=jnp.float32)
-    return part_a, part_b
+F32, BF16 = jnp.float32, jnp.bfloat16
+NT = (((1,), (1,)), ((), ()))
+TN = (((0,), (0,)), ((), ()))
+ROOT = 0.7978845608028654
+CUBE = 0.044715
+
+
+def dot(a, b, dims=(((1,), (0,)), ((), ()))):
+    return lax.dot_general(a, b, dims, preferred_element_type=F32)
+
+
+def compute_kernel(nb1, nb3, grp, x_hbm, lab_hbm, w1_hbm, w2_hbm, a_hbm, bm_hbm, hd_hbm, pb_ref, pa_ref, x, lab, w1, w2, a, bm, hd, h, slope, dz, ut, sem, sem1, sem2):
+    num_tok, d_model = x.shape
+    d_ff = h.shape[1]
+    tasks, _, classes = hd.shape
+    rank = bm.shape[0]
+    n1, n3 = d_ff // nb1, d_ff // nb3
+    small = [(x_hbm, x), (a_hbm, a), (bm_hbm, bm)]
+    late = [(hd_hbm, hd), (lab_hbm, lab)]
+    first = [pltpu.make_async_copy(s, d, sem.at[i]) for i, (s, d) in enumerate(small)]
+    col = [pltpu.make_async_copy(w1_hbm.at[:, i * nb1 : (i + 1) * nb1], w1.at[i], sem1.at[i]) for i in range(n1)]
+    row = [pltpu.make_async_copy(w2_hbm.at[i * nb1 : (i + 1) * nb1], w2.at[i * nb1 : (i + 1) * nb1], sem2.at[i]) for i in range(n1)]
+    last = [pltpu.make_async_copy(s, d, sem.at[3 + i]) for i, (s, d) in enumerate(late)]
+    for c in first + col + last + row:
+        c.start()
+    for c in first:
+        c.wait()
+    xv = x[...]
+    low = dot(xv, a[...])
+    u = low.astype(BF16)
+    ut[...] = jnp.transpose(low).astype(BF16)
+
+    def forward(i, carry):
+        pltpu.make_async_copy(w1_hbm.at[:, pl.ds(pl.multiple_of(i * nb1, nb1), nb1)], w1.at[i], sem1.at[i]).wait()
+        cols = pl.ds(pl.multiple_of(i * nb1, nb1), nb1)
+        p = dot(x[...], w1[i]) + dot(u, bm[:, cols])
+        sq = p * p
+        t = jnp.tanh(ROOT * p * (1.0 + CUBE * sq))
+        cdf = 0.5 + 0.5 * t
+        h[:, cols] = (p * cdf).astype(BF16)
+        slope[:, cols] = cdf + (0.5 * p) * (1.0 - t * t) * (ROOT + (3.0 * CUBE * ROOT) * sq)
+        return carry
+
+    lax.fori_loop(0, n1, forward, 0)
+    for c in row + last:
+        c.wait()
+    z = (x[...].astype(F32) + dot(h[...], w2[...])).astype(BF16)
+    per_task = [jnp.transpose(hd[t].astype(F32)) for t in range(tasks)]
+    head_rows = jnp.concatenate([per_task[t][c : c + 1] for c in range(classes) for t in range(tasks)], axis=0)
+    heads = head_rows.astype(BF16)
+    logits = dot(heads, z, NT)
+    cls = [logits[c * tasks : (c + 1) * tasks] for c in range(classes)]
+    top = functools.reduce(jnp.maximum, cls)
+    ex = [jnp.exp(v - top) for v in cls]
+    tot = functools.reduce(jnp.add, ex)
+    labels = lab[...]
+    err = jnp.concatenate([e / tot - (labels == c).astype(F32) for c, e in enumerate(ex)], axis=0)
+    err = jnp.transpose(err).astype(BF16)
+    own = lax.rem(lax.broadcasted_iota(jnp.int32, head_rows.shape, 0), tasks)
+    for t in range(tasks):
+        dz[t * num_tok : (t + 1) * num_tok] = dot(err, jnp.where(own == t, head_rows, 0.0).astype(BF16)).astype(BF16)
+
+    def backward(i, dlow):
+        cols = pl.ds(pl.multiple_of(i * nb3, nb3), nb3)
+        wb = w2[cols, :]
+        sl = slope[:, cols]
+        new = []
+        for g in range(0, tasks, grp):
+            dh = dot(dz[g * num_tok : (g + grp) * num_tok], wb, NT)
+            for t in range(g, g + grp):
+                dp = (dh[(t - g) * num_tok : (t - g + 1) * num_tok] * sl).astype(BF16)
+                pb_ref[pl.ds(t * rank, rank), cols] = dot(ut[...], dp)
+                new.append(dlow[t] + dot(bm[:, cols], dp, NT))
+        return tuple(new)
+
+    dlow = lax.fori_loop(0, n3, backward, tuple(jnp.zeros((rank, num_tok), F32) for _ in range(tasks)))
+    pa_ref[...] = dot(jnp.concatenate(dlow, axis=0).astype(BF16), x[...])
+
+
+def local_grads(tokens, labels, w_one, w_two, adapter_a, adapter_b, task_heads, nb1=1536, nb3=1536, grp=2):
+    num_tok, d_model = tokens.shape
+    d_ff = w_one.shape[1]
+    tasks, _, classes = task_heads.shape
+    rank = adapter_b.shape[0]
+    dma = pltpu.SemaphoreType.DMA
+    n1 = d_ff // nb1
+    return pl.pallas_call(
+        functools.partial(compute_kernel, nb1, nb3, grp),
+        out_shape=(jax.ShapeDtypeStruct((tasks * rank, d_ff), F32), jax.ShapeDtypeStruct((tasks * rank, d_model), F32)),
+        in_specs=[pl.BlockSpec(memory_space=pl.ANY)] * 7,
+        out_specs=[pl.BlockSpec(memory_space=pltpu.VMEM)] * 2,
+        scratch_shapes=[
+            pltpu.VMEM(tokens.shape, BF16),
+            pltpu.VMEM(labels.shape, jnp.int32),
+            pltpu.VMEM((n1, d_model, nb1), BF16),
+            pltpu.VMEM(w_two.shape, BF16),
+            pltpu.VMEM(adapter_a.shape, BF16),
+            pltpu.VMEM(adapter_b.shape, BF16),
+            pltpu.VMEM(task_heads.shape, BF16),
+            pltpu.VMEM((num_tok, d_ff), BF16),
+            pltpu.VMEM((num_tok, d_ff), F32),
+            pltpu.VMEM((tasks * num_tok, d_model), BF16),
+            pltpu.VMEM((rank, num_tok), BF16),
+            dma((5,)),
+            dma((n1,)),
+            dma((n1,)),
+        ],
+        name="local_grads",
+    )(tokens, labels, w_one, w_two, adapter_a, adapter_b, task_heads)
 
 
 def remote(src, dst, send_sem, recv_sem, dev):
@@ -215,9 +306,7 @@
     def device_step(tokens, labels, w_one, w_two, adapter_a, adapter_b, task_heads):
         batch_total = tokens.shape[0] * num_dev
         tasks = task_heads.shape[0]
-        part_a, part_b = task_grads(tokens, labels, w_one, w_two, adapter_a, adapter_b, task_heads)
-        part_a = part_a.reshape(-1, part_a.shape[2])
-        part_b = part_b.reshape(-1, part_b.shape[2])
+        part_b, part_a = local_grads(tokens, labels, w_one, w_two, adapter_a, adapter_b, task_heads)
         alpha, grad_a, grad_b = exchange(part_b, part_a, DIMS, tasks, batch_total)
         return alpha.reshape(tasks), grad_a, grad_b
 

time: 93.6 us -> 71.5 us (0.76)
  matrix products: 54.8 us -> 0 us
  Pallas kernels: 34.1 us -> 63.6 us
  local copies, waits for them, and re-layouts: 3.68 us -> 7.08 us
    dot_general x7 -> x0, matrix products: 54.8 us -> none  [the longest x1 17.3 us: task_grads(): jnp.einsum('tbd,fd->tbf', d_trunk, w_two, preferred_element_type=jnp.floa...]
    pallas_call x0 -> x1, Pallas kernels: none -> 29.7 us  [local_grads(): pl.pallas_call(functools.partial(compute_kernel, nb1, nb3, grp), out_shap...]
    unnamed x11 -> x5, local copies, waits for them, and re-layouts: 3.68 us -> 7.08 us
where the time goes in v2:
time: 71.5 us; the launch traced here: 71.3 us
  Pallas kernels  63.6 us (89%)
  local copies, waits for them, and re-layouts  7.08 us (10%)
    pallas_call x1, Pallas kernels, exchange(): pl.pallas_call(functools.partial(exchange_kernel, dims, tasks, batch_tota...  33.9 us
    pallas_call x1, Pallas kernels, local_grads(): pl.pallas_call(functools.partial(compute_kernel, nb1, nb3, grp), out_shap...  29.7 us
    unnamed x5, local copies, waits for them, and re-layouts  7.08 us

profile of v2, /device:TPU:1, one launch (start us, length us, event | category | flops | bytes accessed | tf_op | source)
XLA Modules:
  0.0 71.3 jit_solution(2864139966029695784)
XLA Ops:
  0.6 1.5 %copy.10.a_hbm = bf16[768,8]{1,0:T(8,128)(2,1)} copy(bf16[768,8]{0,1:T(8,128)(2,1)} %param.11) | data formatting | bytes 24576 | tf_op args[4]
  2.1 1.9 %copy.11.hd_hbm = bf16[4,768,3]{2,1,0:T(8,128)(2,1)} copy(bf16[4,768,3]{1,0,2:T(4,128)(2,1)} %param.13) | data formatting | bytes 36864 | tf_op args[6]
  4.1 29.7 %local_grads.1 = (f32[32,3072]{1,0:T(8,128)}, f32[32,768]{1,0:T(8,128)}) custom-call(bf16[512,768]{1,0:T(8,128)(2,1)} %x_hbm.1, s32[4,512]{1,0:T(4,128)} %lab_hbm.1, bf16[768,3072]{1,0:T(8,128)(2,1)} %w1_hbm.1, bf16[3072,768]{1,0:T(8,128)(2,1)} %w2_hbm.1, bf16[768,8]{1,0:T(8,128)(2,1)} %copy.10.a_hbm, bf16[8,3072]{1,0:T(8,128)(2,1)} %bm_hbm.1, ...), custom_call_target="tpu_custom_call" | custom-call | tf_op jit(solution)/shard_map/local_grads/pallas_call | solution.py:103
  33.8 33.9 %exchange.1 = (f32[1,4]{1,0:T(1,128)}, f32[3,8]{1,0:T(4,128)}, f32[8,12]{1,0:T(8,128)}) custom-call(f32[32,3072]{1,0:T(8,128)} %get-tuple-element.8.pb_ref, f32[32,768]{1,0:T(8,128)} %get-tuple-element.9.pa_ref), custom_call_target="tpu_custom_call" | custom-call | tf_op jit(solution)/shard_map/exchange/pallas_call | solution.py:273
  67.7 1.1 %copy.15 = f32[4]{0:T(128)} copy(f32[4]{0:T(128)} %bitcast.1) | data formatting | bytes 32
  68.8 1.3 %copy.16 = f32[3,8]{1,0:T(4,128)} copy(f32[3,8]{1,0:T(4,128)} %get-tuple-element.17) | data formatting | bytes 192
  70.0 1.3 %copy.17 = f32[8,12]{1,0:T(8,128)} copy(f32[8,12]{1,0:T(8,128)} %get-tuple-element.18) | data formatting | bytes 768
